TPU v7x, 32 devices: a whole 2x2x4 slice. The times are simulated.
32 devices in a mesh: region: 8 (over z, x), member: 4 (over y, core).
Axes of the slice: x: 2, y: 2, z: 4, core: 2. Of those that a mesh axis runs over, the one named last changes fastest.
Arguments:
- members: float32 [256, 128, 1024], P('member', 'region'), may hold values from -6 to 6
- obs_value: float32 [128, 1024], P('region'), may hold values from -6 to 6
- obs_precision: float32 [128, 1024], P('region'), may hold values from 0.02 to 200
- obs_index: int32 [128, 1024], P('region'), may hold values from 0 to 1023, as said below
- obs_count: int32 [128], P('region'), may hold values from 256 to 1024
Outputs:
- analysis: float32 [256, 128, 1024], P('member', 'region')
Inputs may be any that keep to these rules, and one draw needn't show every extreme that they name: `obs_count`: slots of a tile from its count onward are empty. `obs_index`: position within its own tile.
All inputs are finite; a program needn't handle non-finite values.
Results may differ from a plain program's by a relative error of at most 0.0005.
Values sent between devices are 32-bit elements; how exact they have to be, the bound alone decides.
A program may use at most 64 MiB of HBM per device.

v0:
```python
import math

import jax
import jax.numpy as jnp
from jax import lax
from jax.sharding import PartitionSpec as P

K = 256
ITERS = 12


def extended(block, sides, width):
    for axis, dim in sides:
        count = lax.axis_size(axis)
        forward = [(i, i + 1) for i in range(count - 1)]
        forward.append((count - 1, 0))
        backward = [(target, source) for source, target in forward]
        low = lax.ppermute(
            lax.slice_in_dim(block, block.shape[dim] - width, None, axis=dim), axis, forward
        )
        high = lax.ppermute(lax.slice_in_dim(block, 0, width, axis=dim), axis, backward)
        block = jnp.concatenate([low, block, high], axis=dim)
    return block


def observe(states, places, observed, accuracy, filled):
    average = jnp.sum(states, axis=0) / K
    deviation = states - average[None]
    sampled = jnp.take_along_axis(deviation, places[None], axis=2)
    baseline = jnp.take_along_axis(average, places, axis=1)
    slot_ids = jnp.arange(places.shape[1], dtype=jnp.int32)
    active = slot_ids[None, :] < filled[:, None]
    weight_root = jnp.where(active, jnp.sqrt(accuracy), jnp.float32(0.0))
    scaled = sampled * weight_root[None]
    innov_row = (weight_root * (observed - baseline))[None]
    stacked = jnp.concatenate([scaled, innov_row], axis=0)
    return (average, deviation, stacked)


def outer_gram(stacked):
    return jnp.einsum("ibo,jbo->bij", stacked, stacked, precision=lax.Precision.HIGHEST)


def transform_weights(gram_matrix):
    ensemble = gram_matrix.shape[1] - 1
    identity = jnp.eye(ensemble, dtype=jnp.float32)
    system = (ensemble - 1.0) * identity + gram_matrix[:, :ensemble, :ensemble]
    right_side = gram_matrix[:, :ensemble, ensemble]
    factor = jnp.sqrt(jnp.sum(system * system, axis=(1, 2)) + 1e-06)
    root_iter = system / factor[:, None, None]
    inverse_iter = jnp.broadcast_to(identity, system.shape)

    def one_sweep(sweep_no, iterates):
        root_now, inverse_now = iterates
        middle = 3.0 * identity - jnp.einsum(
            "bij,bjk->bik", inverse_now, root_now, precision=lax.Precision.HIGHEST
        )
        root_next = 0.5 * jnp.einsum(
            "bij,bjk->bik", root_now, middle, precision=lax.Precision.HIGHEST
        )
        inverse_next = 0.5 * jnp.einsum(
            "bij,bjk->bik", middle, inverse_now, precision=lax.Precision.HIGHEST
        )
        return (root_next, inverse_next)

    root_iter, inverse_iter = lax.fori_loop(0, ITERS, one_sweep, (root_iter, inverse_iter))
    inverse_root = inverse_iter / jnp.sqrt(factor)[:, None, None]
    pulled = jnp.einsum("bij,bj->bi", inverse_root, right_side, precision=lax.Precision.HIGHEST)
    shifted = jnp.einsum("bij,bj->bi", inverse_root, pulled, precision=lax.Precision.HIGHEST)
    return math.sqrt(ensemble - 1.0) * inverse_root + shifted[:, :, None]


def analyse(average, deviation, gram_matrix):
    weights = transform_weights(gram_matrix)
    return average[None] + jnp.einsum(
        "jbc,bjk->kbc", deviation, weights, precision=lax.Precision.HIGHEST
    )


def shards(members, obs_value, obs_precision, obs_index, obs_count):
    owned = members.shape[1] // lax.axis_size("member")
    first_band = lax.axis_index("member") * owned
    gathered_states = lax.all_to_all(members, "member", split_axis=1, concat_axis=0, tiled=True)

    def own_rows(tables):
        return lax.dynamic_slice_in_dim(tables, first_band, owned, 0)

    average, deviation, stacked = observe(
        gathered_states,
        own_rows(obs_index),
        own_rows(obs_value),
        own_rows(obs_precision),
        own_rows(obs_count),
    )
    beside_all = extended(outer_gram(stacked)[None], (("region", 0),), 1)
    gram_matrix = beside_all[1] + 0.5 * (beside_all[0] + beside_all[2])
    result = analyse(average, deviation, gram_matrix)
    return lax.all_to_all(result, "member", split_axis=0, concat_axis=1, tiled=True)


def solution(mesh):
    in_specs = (
        P("member", "region", None),
        P("region", None),
        P("region", None),
        P("region", None),
        P("region"),
    )
    out_specs = P("member", "region", None)
    return jax.shard_map(shards, mesh=mesh, in_specs=in_specs, out_specs=out_specs, check_vma=False)
```

profile of v0, /device:TPU:0, one launch (start us, length us, event | category | flops | bytes accessed | tf_op | source)
XLA Modules:
  0.0 407.7 jit_solution(212187878441169337)
XLA Ops:
  0.0 6.6 %copy.37 = f32[64,16,1024]{2,0,1:T(8,128)} copy(f32[64,16,1024]{2,1,0:T(8,128)} %param.7) | data formatting | bytes 8388608 | tf_op args[0]
  6.6 5.2 %all-to-all-start = ((f32[64,16,1024]{2,0,1:T(8,128)}), f32[64,16,1024]{2,0,1:T(8,128)}, u32[]{:S(2)}, u32[]{:S(2)}) async-start(f32[64,16,1024]{2,0,1:T(8,128)} %copy.37), calls=%async_computation | async-start | bytes 8388608 | tf_op jit(solution)/shard_map/all_to_all | solution.py:83
  11.9 48.8 %all-to-all-done = f32[64,16,1024]{2,0,1:T(8,128)} async-done(((f32[64,16,1024]{2,0,1:T(8,128)}), f32[64,16,1024]{2,0,1:T(8,128)}, u32[]{:S(2)}, u32[]{:S(2)}) %all-to-all-start) | async-done | bytes 4194336 | tf_op jit(solution)/shard_map/all_to_all | solution.py:83
  60.7 4.8 %copy.38 = f32[4,64,4,1024]{3,1,0,2:T(8,128)} copy(f32[4,64,4,1024]{3,1,2,0:T(8,128)} %bitcast.1) | data formatting | bytes 8388608 | tf_op jit(solution)/shard_map/all_to_all | solution.py:83
  65.5 2.5 reduce_sum.18
  68.0 34.9 %gather_fusion.1 = f32[4096]{0:T(1024)S(1)} fusion(f32[4,1024]{1,0:T(4,128)S(1)} %broadcast_multiply_fusion, s32[4096]{0:T(1024)S(1)} %bitcast.55), kind=kCustom, calls=%fused_computation.1 | custom fusion | bytes 65536 | tf_op jit(solution)/shard_map/jit(take_along_axis)/gather | solution.py:30
  102.9 5.4 %copy.39 = f32[256,4,1024]{0,2,1:T(8,128)} copy(f32[256,4,1024]{2,0,1:T(8,128)} %bitcast.58) | data formatting | bytes 8388608 | tf_op jit(solution)/shard_map/all_to_all | solution.py:83
  108.3 3.9 broadcast_subtract_fusion
  112.3 73.6 %gather_fusion = f32[4096,256]{1,0:T(8,128)} fusion(f32[256,4,1024]{0,2,1:T(8,128)} %broadcast_subtract_fusion, s32[4096]{0:T(1024)S(1)} %bitcast.56), kind=kCustom, calls=%fused_computation | custom fusion | bytes 8421376 | tf_op jit(solution)/shard_map/jit(take_along_axis)/gather | solution.py:29
  185.9 5.3 %copy.40 = f32[4,1024,256]{1,2,0:T(8,128)} copy(f32[4,1024,256]{2,1,0:T(8,128)} %bitcast.57) | data formatting | bytes 8388608 | tf_op jit(solution)/shard_map/jit(take_along_axis)/gather | solution.py:29
  192.1 2.7 multiply_bitcast_fusion
  194.8 6.8 %fusion.4 = f32[4,257,257]{1,2,0:T(8,128)S(1)} fusion(f32[1,4,1024]{2,0,1:T(1,128)S(1)} %broadcast_in_dim.40, f32[256,4,1024]{2,0,1:T(8,128)S(1)} %multiply_bitcast_fusion), kind=kOutput, calls=%fused_computation.9 | convolution fusion | flops 3247493120 | bytes 5267472 | tf_op jit(solution)/shard_map/ibo,jbo->bij/dot_general | solution.py:41
  201.7 2.3 copy.41
  204.9 3.8 collective-permute-start.1
  209.6 62.6 %collective-permute-done = f32[1,4,257,257]{3,1,2,0:T(4,128)} collective-permute-done((f32[1,4,257,257]{3,1,2,0:T(4,128)}, f32[1,4,257,257]{3,1,2,0:T(4,128)}, u32[]{:S(2)}, u32[]{:S(2)}) %collective-permute-start) | collective-permute-done | bytes 1056816 | tf_op jit(solution)/shard_map/ppermute | solution.py:18
  272.2 2.7 copy.43
  275.5 3.6 copy.44
  282.1 53.2 %while.13 = (s32[]{:T(128)}, f32[4,256,256]{1,2,0:T(8,128)S(1)}, f32[4,256,256]{2,1,0:T(8,128)S(1)}, s32[]{:T(128)}) while((s32[]{:T(128)}, f32[4,256,256]{1,2,0:T(8,128)S(1)}, f32[4,256,256]{2,1,0:T(8,128)S(1)}, s32[]{:T(128)}) %tuple.24), condition=%wide.region_3.4_spmd.clone, body=%wide.region_2.3_spmd.clone.sunk | while | flops 2416836608 | bytes 14155829 | solution.py:66
  284.6 1.9 fusion.44
  289.0 1.9 fusion.44
  293.4 1.9 fusion.44
  297.9 1.9 fusion.44
  302.3 1.9 fusion.44
  306.7 1.9 fusion.44
  311.1 1.9 fusion.44
  333.3 1.9 fusion.44
  335.2 2.0 fusion.16
  338.3 7.8 %add_bitcast_fusion = f32[256,4,1024]{2,0,1:T(8,128)S(1)} fusion(f32[4,1024]{1,0:T(4,128)S(1)} %broadcast_multiply_fusion, f32[4,256]{1,0:T(4,128)S(1)} %bitcast.61, f32[4,256,256]{2,1,0:T(8,128)S(1)} %get-tuple-element.27, f32[4]{0:T(128)S(1)} %get-tuple-element.45, f32[256,4,1024]{0,2,1:T(8,128)S(1)} %copy-done), kind=kOutput, calls=%fused_computation.14 | convolution fusion | flops 3224109056 | bytes 9457680 | tf_op jit(solution)/shard_map/jbc,bjk->kbc/dot_general | solution.py:75
  346.1 2.7 copy.48
  348.9 50.7 %all_to_all.36 = f32[256,4,1024]{2,1,0:T(4,128)S(1)} all-to-all(f32[256,4,1024]{2,1,0:T(4,128)S(1)} %copy.48), channel_id=1, replica_groups=mesh['region'=8,'member'=4] {'member'}, dimensions={0} | all-to-all | bytes 8388608 | tf_op jit(solution)/shard_map/all_to_all | solution.py:98
  399.6 2.9 copy.49
  402.5 5.3 %all_to_all.33 = f32[64,16,1024]{2,1,0:T(8,128)} reshape(f32[64,4,4,1024]{3,2,1,0:T(4,128)} %copy.49) | data formatting | bytes 8388608 | tf_op jit(solution)/shard_map/all_to_all | solution.py:98
  (94 shorter events, 44.5 us)
Async XLA Ops:
  6.6 5.2 %copy-start.3 = (s32[16,1024]{1,0:T(8,128)S(1)}, s32[16,1024]{1,0:T(8,128)}, u32[]{:S(2)}) copy-start(s32[16,1024]{1,0:T(8,128)} %param.10) | copy-start | bytes 196612
  6.6 5.2 %copy-start.4 = (s32[16]{0:T(128)S(1)}, s32[16]{0:T(128)}, u32[]{:S(2)}) copy-start(s32[16]{0:T(128)} %param.11) | copy-start | bytes 196
  6.6 54.1 %all-to-all-start = ((f32[64,16,1024]{2,0,1:T(8,128)}), f32[64,16,1024]{2,0,1:T(8,128)}, u32[]{:S(2)}, u32[]{:S(2)}) async-start(f32[64,16,1024]{2,0,1:T(8,128)} %copy.37), calls=%async_computation | async-start | bytes 8388608 | tf_op jit(solution)/shard_map/all_to_all | solution.py:83
  204.0 68.2 %collective-permute-start = (f32[1,4,257,257]{3,1,2,0:T(4,128)}, f32[1,4,257,257]{3,1,2,0:T(4,128)}, u32[]{:S(2)}, u32[]{:S(2)}) collective-permute-start(f32[1,4,257,257]{3,1,2,0:T(4,128)} %copy.41), channel_id=1, source_target_pairs={{0,4},{4,8},{8,12},{12,16},{16,20},{20,24},{24,28},{28,0},{1,5},{5... | collective-permute-start | bytes 3170360 | tf_op jit(solution)/shard_map/ppermute | solution.py:18
  204.9 70.6 %collective-permute-start.1 = (f32[1,4,257,257]{3,1,2,0:T(4,128)}, f32[1,4,257,257]{3,1,2,0:T(4,128)}, u32[]{:S(2)}, u32[]{:S(2)}) collective-permute-start(f32[1,4,257,257]{3,1,2,0:T(4,128)} %copy.41), channel_id=1, source_target_pairs={{4,0},{8,4},{12,8},{16,12},{20,16},{24,20},{28,24},{0,28},{5,1},{9... | collective-permute-start | bytes 3170360 | tf_op jit(solution)/shard_map/ppermute | solution.py:21
  280.8 1.2 copy-start.1
  280.8 1.1 copy-start.2
  335.2 3.1 copy-start
where the time goes:
time: 409 us; the launch traced here: 408 us
  local copies, waits for them, and re-layouts  154 us (38%)
  waiting for transfers between devices  112 us (27%)
  matrix products  68.2 us (17%)
  blocking collectives  50.7 us (12%)
  other arithmetic  12.4 us (3%)
  starting transfers between devices  9.88 us (2%)
    gather x2, local copies, waits for them, and re-layouts, observe(): sampled = jnp.take_along_axis(deviation, places[None], axis=2)  79 us
    ppermute x1, waiting for transfers between devices, extended(): lax.ppermute(lax.slice_in_dim(block, block.shape[dim] - width, None, axis...  62.6 us
    all_to_all x1, blocking collectives, shards(): lax.all_to_all(result, 'member', split_axis=0, concat_axis=1, tiled=True)  50.7 us
    all_to_all x1, waiting for transfers between devices, shards(): lax.all_to_all(members, 'member', split_axis=1, concat_axis=0, tiled=True)  48.8 us
    gather x2, local copies, waits for them, and re-layouts, observe(): baseline = jnp.take_along_axis(average, places, axis=1)  34.9 us
    dot_general x12, matrix products, one_sweep(): jnp.einsum('bij,bjk->bik', root_now, middle, precision=lax.Precision.HIGH...  22.9 us
    dot_general x12, matrix products, one_sweep(): jnp.einsum('bij,bjk->bik', inverse_now, root_now, precision=lax.Precision...  13.8 us
    dot_general x12, matrix products, one_sweep(): jnp.einsum('bij,bjk->bik', middle, inverse_now, precision=lax.Precision.H...  13.7 us
  transfers between devices with their start and end apart: 3, of which 3 were waited for; matrix products, arithmetic and copies ran while one was open for 1% of the time, Pallas kernels for 0%

commit v1 on v0

v1 whole, which is shorter than its diff:
```python
import functools
import math

import jax
import jax.numpy as jnp
from jax import lax
from jax.experimental import pallas as pl
from jax.experimental.pallas import tpu as pltpu
from jax.sharding import PartitionSpec as P

ITERS = 12
LANES = 128
F32 = jnp.float32
BF16 = jnp.bfloat16


def split3(x):
    a = x.astype(BF16)
    rest = x - a.astype(F32)
    b = rest.astype(BF16)
    return a, b, (rest - b.astype(F32)).astype(BF16)


def dot(a, b):
    return jnp.dot(a, b, preferred_element_type=F32)


def dot_nt(a, b):
    return lax.dot_general(a, b, (((1,), (1,)), ((), ())), preferred_element_type=F32)


def product(a, b):
    a1, a2, a3 = a
    b1, b2, b3 = b
    left = jnp.concatenate([a1, a3, a2, a1, a2, a1], axis=1)
    right = jnp.concatenate([b3, b1, b2, b2, b1, b1], axis=0)
    return dot(left, right)


def gram_kernel(x_ref, index_ref, value_ref, precision_ref, out_ref):
    states = x_ref[0]
    size, width = states.shape
    half = size // 2
    groups = width // LANES
    places, exact = index_ref[0], precision_ref[0]
    slots = places.shape[1]

    high = lax.shift_right_logical(places, 7)
    low = lax.bitwise_and(places, LANES - 1)
    rows = lax.broadcasted_iota(jnp.int32, (groups, slots), 0) == high
    both = jnp.concatenate(
        [jnp.where(rows, exact, 0.0), jnp.where(rows, exact * value_ref[0], 0.0)], axis=0
    )
    one_hot = jnp.where(
        lax.broadcasted_iota(jnp.int32, (LANES, slots), 0) == low, 1.0, 0.0
    ).astype(BF16)
    e1, e2, e3 = split3(both)
    sums = dot_nt(e3, one_hot) + dot_nt(e2, one_hot) + dot_nt(e1, one_hot)
    c = jnp.concatenate([sums[i : i + 1] for i in range(groups)], axis=1)
    d = jnp.concatenate([sums[groups + i : groups + i + 1] for i in range(groups)], axis=1)

    average = jnp.sum(states, axis=0, keepdims=True) / size
    deviation = states - average
    s1, s2, s3 = split3(deviation * jnp.sqrt(c))
    cross = dot_nt(s1, s3) + dot_nt(s1, s2)
    own = (dot_nt(s2, s2) + (cross + cross.T)) + dot_nt(s1, s1)

    pulled = deviation * (d - c * average)
    folded = pulled[:, :LANES]
    for i in range(1, groups):
        folded = folded + pulled[:, i * LANES : (i + 1) * LANES]
    right = jnp.sum(folded.T, axis=0, keepdims=True)

    row = lax.broadcasted_iota(jnp.int32, (half, half), 0)
    col = lax.broadcasted_iota(jnp.int32, (half, half), 1)
    first, last = own[:half, :half], own[half:, half:]
    diagonal = jnp.sum(jnp.where(row == col, last, 0.0), axis=0, keepdims=True)
    out_ref[0, :half, :half] = own[:half, half:]
    out_ref[0, :half, half:] = jnp.where(row <= col, first, last)
    tail = jnp.concatenate([right, jnp.concatenate([diagonal, diagonal], axis=1)], axis=0)
    out_ref[0, half:, :] = jnp.concatenate([tail, jnp.zeros((6, size), F32)], axis=0)


def analysis_kernel(own_ref, west_ref, east_ref, x_ref, out_ref, u_ref, z_ref):
    tiles, size, width = x_ref.shape
    half = size // 2
    row = lax.broadcasted_iota(jnp.int32, (size, size), 0)
    col = lax.broadcasted_iota(jnp.int32, (size, size), 1)
    identity = jnp.where(row == col, 1.0, 0.0).astype(F32)
    small_row, small_col = row[:half, :half], col[:half, :half]
    rights, scales = [], []

    def growth(u, z):
        x = split3(u if z is None else product(z, u))
        plain = u if z is None else x[0].astype(F32) + x[1].astype(F32) + x[2].astype(F32)
        squared = product(x, x)
        inner = (1 / 16) * squared - (9 / 16) * plain
        outer = product(split3(squared), split3(inner))
        return (36 / 16) * identity - (39 / 16) * plain + (27 / 16) * squared + outer

    for t in range(tiles):
        packed = own_ref[t] + 0.5 * (west_ref[t] + east_ref[t])
        upper, mixed = packed[:half, :half], packed[:half, half:]
        rights.append(packed[half : half + 1])
        diagonal = packed[half + 1 : half + 2, :half]
        turned = mixed.T
        first = jnp.where(small_row <= small_col, mixed, turned)
        last = jnp.where(small_row > small_col, mixed, turned)
        last = jnp.where(small_row == small_col, diagonal, last)
        gram = jnp.concatenate(
            [
                jnp.concatenate([first, upper], axis=1),
                jnp.concatenate([upper.T, last], axis=1),
            ],
            axis=0,
        )
        system = (size - 1.0) * identity + gram
        total = jnp.sum(jnp.sum(system * system, axis=0, keepdims=True), axis=1, keepdims=True)
        scale = jnp.sqrt(total + 1e-6)
        scales.append(scale)
        u = system / scale
        g = growth(u, None)
        z_ref[t] = g
        u_ref[t] = product(split3(u), split3(g))

    def two_steps(_, carry):
        for t in range(tiles):
            u, z = split3(u_ref[t]), split3(z_ref[t])
            g = split3(growth(u, z))
            u_ref[t] = product(u, g)
            z_ref[t] = product(g, z)
        return carry

    lax.fori_loop(0, ITERS // 2 - 2, two_steps, 0)

    for t in range(tiles):
        u, z = split3(u_ref[t]), split3(z_ref[t])
        inverse = product(split3(growth(u, z)), z) / jnp.sqrt(scales[t])
        pulled = jnp.sum(inverse * rights[t], axis=1, keepdims=True)
        shift = jnp.sum(inverse * pulled, axis=0, keepdims=True)
        weights = math.sqrt(size - 1.0) * inverse + shift
        average = jnp.sum(x_ref[t], axis=0, keepdims=True) / size
        w1, w2, _ = split3(weights)
        d1, d2, _ = split3(x_ref[t] - average)
        left = jnp.concatenate([w2, w1, w1], axis=1)
        right = jnp.concatenate([d1, d2, d1], axis=0)
        out_ref[t] = average + dot(left, right)


def block(*shape):
    return pl.BlockSpec(shape, lambda i: (i,) + (0,) * (len(shape) - 1))


def grams(states, places, observed, accuracy):
    owned, size, width = states.shape
    slots = places.shape[1]
    table = block(1, 1, slots)
    return pl.pallas_call(
        gram_kernel,
        grid=(owned,),
        in_specs=[block(1, size, width), table, table, table],
        out_specs=block(1, size // 2 + 8, size),
        out_shape=jax.ShapeDtypeStruct((owned, size // 2 + 8, size), F32),
        cost_estimate=pl.CostEstimate(
            flops=owned * 12 * size * size * width, bytes_accessed=states.size * 4, transcendentals=0
        ),
    )(states, places[:, None], observed[:, None], accuracy[:, None])


def analyses(own, west, east, states):
    owned, size, width = states.shape
    tiles = 2 if owned % 2 == 0 else 1
    packed = block(tiles, size // 2 + 8, size)
    return pl.pallas_call(
        analysis_kernel,
        grid=(owned // tiles,),
        in_specs=[packed, packed, packed, block(tiles, size, width)],
        out_specs=block(tiles, size, width),
        out_shape=jax.ShapeDtypeStruct(states.shape, F32),
        scratch_shapes=[pltpu.VMEM((tiles, size, size), F32)] * 2,
        cost_estimate=pl.CostEstimate(
            flops=owned * 27 * 12 * size**3, bytes_accessed=states.size * 8, transcendentals=0
        ),
        compiler_params=pltpu.CompilerParams(vmem_limit_bytes=56 * 2**20),
    )(own, west, east, states)


def shards(chunks, members, obs_value, obs_precision, obs_index, obs_count):
    owned = members.shape[1] // lax.axis_size("member")
    parts = chunks if owned % chunks == 0 else 1
    first_band = lax.axis_index("member") * owned
    per = owned // parts
    count = lax.axis_size("member")
    rows, tiles, width = members.shape

    def own_rows(tables):
        return lax.dynamic_slice_in_dim(tables, first_band, owned, 0)

    filled = own_rows(obs_count)
    slot_ids = jnp.arange(obs_value.shape[1], dtype=jnp.int32)
    accuracy = jnp.where(slot_ids[None] < filled[:, None], own_rows(obs_precision), 0.0)
    places, observed = own_rows(obs_index), own_rows(obs_value)

    turned = members.reshape(rows, count, parts, per, width).transpose(2, 1, 3, 0, 4)
    columns = lax.axis_size("region")
    forward = [(i, (i + 1) % columns) for i in range(columns)]
    backward = [(b, a) for a, b in forward]
    gathered, packed = [], []
    for i in range(parts):
        got = lax.all_to_all(turned[i], "member", split_axis=0, concat_axis=0, tiled=False)
        got = got.transpose(1, 0, 2, 3).reshape(per, count * rows, width)
        span = slice(i * per, (i + 1) * per)
        own = grams(got, places[span], observed[span], accuracy[span])
        gathered.append(got)
        packed.append(
            (own, lax.ppermute(own, "region", forward), lax.ppermute(own, "region", backward))
        )
    results = []
    for i in range(parts):
        result = analyses(*packed[i], gathered[i])
        result = result.reshape(per, count, rows, width).transpose(1, 0, 2, 3)
        results.append(lax.all_to_all(result, "member", split_axis=0, concat_axis=0, tiled=False))
    return jnp.stack(results, axis=1).reshape(tiles, rows, width).transpose(1, 0, 2)


def solution(mesh):
    in_specs = (
        P("member", "region", None),
        P("region", None),
        P("region", None),
        P("region", None),
        P("region"),
    )
    out_specs = P("member", "region", None)
    return jax.shard_map(
        functools.partial(shards, 1),
        mesh=mesh,
        in_specs=in_specs,
        out_specs=out_specs,
        check_vma=False,
    )
```

time: 409 us -> 213 us (0.52)
  local copies, waits for them, and re-layouts: 154 us -> 21.7 us
  matrix products: 68.2 us -> 0 us
  Pallas kernels: 0 us -> 61.6 us
  waiting for transfers between devices: 112 us -> 67.8 us
  other arithmetic: 12.4 us -> 0.85 us
    gather x4 -> x0, local copies, waits for them, and re-layouts: 114 us -> none  [the longest x2 79 us: observe(): sampled = jnp.take_along_axis(deviation, places[None], axis=2)]
    dot_general x40 -> x0, matrix products: 68.2 us -> none  [the longest x12 22.9 us: one_sweep(): jnp.einsum('bij,bjk->bik', root_now, middle, precision=lax.Precision.HIGH...]
    pallas_call x0 -> x2, Pallas kernels: none -> 61.6 us  [the longest x1 53.5 us: analyses(): pl.pallas_call(analysis_kernel, grid=(owned // tiles,), in_specs=[packed,...]
    ppermute x2, waiting for transfers between devices: 63.2 us -> 21.7 us  [the longest x1 21.4 us: shards(): lax.ppermute(own, 'region', backward)]
    all_to_all x4 -> x0, local copies, waits for them, and re-layouts: 18.4 us -> none  [the longest x2 10.2 us: shards(): lax.all_to_all(members, 'member', split_axis=1, concat_axis=0, tiled=True)]
    ppermute x2 -> x0, local copies, waits for them, and re-layouts: 6.36 us -> none  [the longest x1 3.63 us: extended(): lax.ppermute(lax.slice_in_dim(block, 0, width, axis=dim), axis, backward)]
    transpose x0 -> x1, local copies, waits for them, and re-layouts: none -> 4.79 us  [shards(): got = got.transpose(1, 0, 2, 3).reshape(per, count * rows, width)]
    another operation x0 -> x1, local copies, waits for them, and re-layouts: none -> 4.44 us  [shards(): jnp.stack(results, axis=1).reshape(tiles, rows, width).transpose(1, 0, 2)]
where the time goes in v1:
time: 213 us
  waiting for transfers between devices  67.8 us (32%)
  Pallas kernels  61.6 us (29%)
  blocking collectives  50.7 us (24%)
  local copies, waits for them, and re-layouts  21.7 us (10%)
  starting transfers between devices  10.3 us (5%)
    pallas_call x1, Pallas kernels, analyses(): pl.pallas_call(analysis_kernel, grid=(owned // tiles,), in_specs=[packed,...  53.5 us
    all_to_all x1, blocking collectives, shards(): lax.all_to_all(result, 'member', split_axis=0, concat_axis=0, tiled=False)  50.7 us
    all_to_all x1, waiting for transfers between devices, shards(): lax.all_to_all(turned[i], 'member', split_axis=0, concat_axis=0, tiled=Fa...  46.1 us
    ppermute x1, waiting for transfers between devices, shards(): lax.ppermute(own, 'region', backward)  21.4 us
    pallas_call x1, Pallas kernels, grams(): pl.pallas_call(gram_kernel, grid=(owned,), in_specs=[block(1, size, width...  8.07 us
    unnamed x9, local copies, waits for them, and re-layouts  8.06 us
    ppermute x1, starting transfers between devices, shards(): lax.ppermute(own, 'region', backward)  5.3 us
    all_to_all x1, starting transfers between devices, shards(): lax.all_to_all(turned[i], 'member', split_axis=0, concat_axis=0, tiled=Fa...  4.97 us
  transfers between devices with their start and end apart: 3, of which 3 were waited for; matrix products, arithmetic and copies ran while one was open for 1% of the time, Pallas kernels for 0%

profile of v1, /device:TPU:0, one launch (start us, length us, event | category | flops | bytes accessed | tf_op | source)
XLA Modules:
  0.0 213.0 jit_solution(7297065657048837653)
XLA Ops:
  0.0 0.0 copy-start
  0.0 6.7 %copy.8 = f32[64,16,1024]{2,0,1:T(8,128)} copy(f32[64,16,1024]{2,1,0:T(8,128)} %param.5) | data formatting | bytes 8388608 | tf_op args[0]
  6.7 0.0 copy-start.3
  6.7 5.0 %all-to-all-start = ((f32[4,4,64,1024]{3,2,1,0:T(8,128)}), f32[4,4,64,1024]{3,2,1,0:T(8,128)}, u32[]{:S(2)}, u32[]{:S(2)}) async-start(f32[4,4,64,1024]{3,2,1,0:T(8,128)} %bitcast.15), calls=%async_computation | async-start | bytes 8388608 | tf_op jit(solution)/shard_map/all_to_all | solution.py:210
  11.6 0.0 copy-done.3
  11.7 0.1 dynamic_slice.14
  11.7 0.0 copy-done
  11.7 0.6 broadcast_in_dim.15.index_ref
  12.4 0.8 dynamic-slice_select_fusion
  13.2 0.6 broadcast_in_dim.18.precision_ref
  13.8 0.6 broadcast_in_dim.16.value_ref
  14.4 46.1 %all-to-all-done = f32[4,4,64,1024]{3,2,1,0:T(8,128)} async-done(((f32[4,4,64,1024]{3,2,1,0:T(8,128)}), f32[4,4,64,1024]{3,2,1,0:T(8,128)}, u32[]{:S(2)}, u32[]{:S(2)}) %all-to-all-start) | async-done | bytes 4194336 | tf_op jit(solution)/shard_map/all_to_all | solution.py:210
  60.5 4.8 %copy.9 = f32[4,4,64,1024]{3,2,1,0:T(8,128)} copy(f32[4,4,64,1024]{3,2,0,1:T(8,128)} %bitcast.3) | data formatting | bytes 8388608 | tf_op jit(solution)/shard_map/transpose | solution.py:211
  65.3 8.1 %shard_map.55.own_ref = f32[4,136,256]{2,1,0:T(8,128)} custom-call(f32[4,256,1024]{2,1,0:T(8,128)} %bitcast.18, s32[4,1,1024]{2,1,0:T(1,128)} %broadcast_in_dim.15.index_ref, f32[4,1,1024]{2,1,0:T(1,128)} %broadcast_in_dim.16.value_ref, f32[4,1,1024]{2,1,0:T(1,128)} %broadcast_in_dim.18.precision_ref), custom_call_target="tpu_custom_call" | custom-call | flops 3221225472 | bytes 4194304 | tf_op jit(solution)/shard_map/pallas_call | solution.py:158
  73.4 5.3 %collective-permute-start.1 = (f32[4,136,256]{2,1,0:T(8,128)}, f32[4,136,256]{2,1,0:T(8,128)S(1)}, u32[]{:S(2)}, u32[]{:S(2)}) collective-permute-start(f32[4,136,256]{2,1,0:T(8,128)} %shard_map.55.own_ref), channel_id=1, source_target_pairs={{4,0},{8,4},{12,8},{16,12},{20,16},{24,20},{28,24},{0,28},{5,1},{9... | collective-permute-start | bytes 1671176 | tf_op jit(solution)/shard_map/ppermute | solution.py:216
  78.7 0.0 collective-permute-start
  78.7 21.4 %collective-permute-done.1.east_ref = f32[4,136,256]{2,1,0:T(8,128)S(1)} collective-permute-done((f32[4,136,256]{2,1,0:T(8,128)}, f32[4,136,256]{2,1,0:T(8,128)S(1)}, u32[]{:S(2)}, u32[]{:S(2)}) %collective-permute-start.1) | collective-permute-done | bytes 557088 | tf_op jit(solution)/shard_map/ppermute | solution.py:216
  100.1 0.0 copy-start.1
  100.2 0.3 collective-permute-done.west_ref
  100.4 0.6 copy-done.1
  101.0 0.0 copy-start.2
  101.0 0.8 copy-done.2
  101.8 53.5 %shard_map.56 = f32[4,256,1024]{2,1,0:T(8,128)} custom-call(f32[4,136,256]{2,1,0:T(8,128)} %shard_map.55.own_ref, f32[4,136,256]{2,1,0:T(8,128)} %copy-done.2, f32[4,136,256]{2,1,0:T(8,128)} %copy-done.1, f32[4,256,1024]{2,1,0:T(8,128)} %bitcast.19), custom_call_target="tpu_custom_call" | custom-call | flops 21743271936 | bytes 8388608 | tf_op jit(solution)/shard_map/pallas_call | solution.py:174
  155.4 2.5 %copy.15 = f32[4,4,64,1024]{3,2,0,1:T(8,128)S(1)} copy(f32[4,4,64,1024]{3,2,1,0:T(8,128)} %bitcast.20) | data formatting | bytes 8388608 | tf_op jit(solution)/shard_map/reshape | solution.py:221
  157.9 50.7 %all_to_all.10 = f32[4,4,64,1024]{3,2,1,0:T(8,128)S(1)} all-to-all(f32[4,4,64,1024]{3,2,1,0:T(8,128)S(1)} %bitcast.16), channel_id=1, replica_groups=mesh['region'=8,'member'=4] {'member'}, dimensions={0} | all-to-all | bytes 8388608 | tf_op jit(solution)/shard_map/all_to_all | solution.py:222
  208.6 4.4 %copy.14 = f32[16,64,1024]{2,0,1:T(8,128)} copy(f32[16,64,1024]{2,1,0:T(8,128)S(1)} %bitcast.17) | data formatting | bytes 8388608 | tf_op jit(solution)/shard_map/reshape;stack | solution.py:223
  (1 shorter events, 0.0 us)
Async XLA Ops:
  0.0 11.7 %copy-start = (s32[16,1024]{1,0:T(8,128)S(1)}, s32[16,1024]{1,0:T(8,128)}, u32[]{:S(2)}) copy-start(s32[16,1024]{1,0:T(8,128)} %param.8) | copy-start | bytes 196612
  6.7 5.0 %copy-start.3 = (s32[16]{0:T(128)S(1)}, s32[16]{0:T(128)}, u32[]{:S(2)}) copy-start(s32[16]{0:T(128)} %param.9) | copy-start | bytes 196
  6.7 53.9 %all-to-all-start = ((f32[4,4,64,1024]{3,2,1,0:T(8,128)}), f32[4,4,64,1024]{3,2,1,0:T(8,128)}, u32[]{:S(2)}, u32[]{:S(2)}) async-start(f32[4,4,64,1024]{3,2,1,0:T(8,128)} %bitcast.15), calls=%async_computation | async-start | bytes 8388608 | tf_op jit(solution)/shard_map/all_to_all | solution.py:210
  73.4 26.7 %collective-permute-start.1 = (f32[4,136,256]{2,1,0:T(8,128)}, f32[4,136,256]{2,1,0:T(8,128)S(1)}, u32[]{:S(2)}, u32[]{:S(2)}) collective-permute-start(f32[4,136,256]{2,1,0:T(8,128)} %shard_map.55.own_ref), channel_id=1, source_target_pairs={{4,0},{8,4},{12,8},{16,12},{20,16},{24,20},{28,24},{0,28},{5,1},{9... | collective-permute-start | bytes 1671176 | tf_op jit(solution)/shard_map/ppermute | solution.py:216
  78.7 21.7 %collective-permute-start = (f32[4,136,256]{2,1,0:T(8,128)}, f32[4,136,256]{2,1,0:T(8,128)S(1)}, u32[]{:S(2)}, u32[]{:S(2)}) collective-permute-start(f32[4,136,256]{2,1,0:T(8,128)} %shard_map.55.own_ref), channel_id=1, source_target_pairs={{0,4},{4,8},{8,12},{12,16},{16,20},{20,24},{24,28},{28,0},{1,5},{5... | collective-permute-start | bytes 1671176 | tf_op jit(solution)/shard_map/ppermute | solution.py:216
  100.1 0.8 copy-start.1
  101.0 0.8 copy-start.2
